TPU v7x, 128 devices: a whole 4x4x4 slice. The times are simulated.
128 devices in a mesh: pair: 16 (over x, z_lo, core), ga: 8 (over z_hi, y).
Axes of the slice: x: 4, y: 4, z: 4 (z_hi: 2, z_lo: 2; z = z_hi * 2 + z_lo), core: 2. Of those that a mesh axis runs over, the one named last changes fastest.
Arguments:
- densities: bfloat16 [24576, 4096], P('pair', 'ga'), may hold values from -6 to 6
- val_band: int32 [24576], P('pair'), may hold values from 0 to 127
- cond_band: int32 [24576], P('pair'), may hold values from 0 to 255
- val_energy: float32 [128], replicated, may hold values from -12 to -1
- cond_energy: float32 [256], replicated, may hold values from 1 to 12
Outputs:
- chi: float32 [4096, 4096], P('ga', 'pair')
All inputs are finite; a program needn't handle non-finite values.
Results may differ from a plain program's by a relative error of at most 0.0012.
Values may be sent and summed in bfloat16 or wider, within the bound.
A program may use at most 128 MiB of HBM per device.

v0:
```python
import math
import jax
import jax.numpy as jnp
from jax import lax
from jax.sharding import PartitionSpec as P


def lookup(bands, table):
    levels = lax.broadcasted_iota(jnp.int32, (1, table.shape[0]), 1)
    onehot = (bands[:, None] == levels).astype(jnp.float32)
    return jnp.sum(onehot * table[None, :], axis=1)


def per_device(densities, val_band, cond_band, val_energy, cond_energy):
    pairs_total = densities.shape[0] * lax.axis_size("pair")
    gap = lookup(val_band, val_energy) - lookup(cond_band, cond_energy)
    weight = 4.0 / (gap * math.sqrt(pairs_total))
    scaled = (weight[:, None] * densities.astype(jnp.float32)).astype(jnp.bfloat16)
    gathered = lax.all_gather(densities, "ga", axis=1, tiled=True)
    owned = lax.psum_scatter(
        lax.dot_general(
            gathered, scaled, (((0,), (0,)), ((), ())), preferred_element_type=jnp.float32
        ),
        "pair",
        scatter_dimension=0,
        tiled=True,
    )
    return owned.T


def solution(mesh):
    placed = (P("pair", "ga"), P("pair"), P("pair"), P(), P())
    return jax.shard_map(
        per_device, mesh=mesh, in_specs=placed, out_specs=P("ga", "pair"), check_vma=False
    )
```

profile of v0, /device:TPU:5, one launch (start us, length us, event | category | flops | bytes accessed | tf_op | source)
XLA Modules:
  0.0 290.0 jit_solution(14027633360789709186)
XLA Ops:
  6.5 0.0 copy-start
  6.5 0.0 copy-start.3
  6.5 0.0 copy-start.2
  6.5 0.0 copy-start.1
  6.5 0.0 all-gather.2.cloned.1.call-start
  6.6 0.7 all-gather.2.cloned.1.call-update
  7.3 0.0 reduce-scatter.2.cloned.1.call-start
  7.3 0.0 copy-done.3
  7.3 1.2 select_reduce_fusion.1
  8.5 0.0 copy-done.2
  8.5 0.0 copy-done.1
  8.5 0.5 select_reduce_fusion
  9.1 163.8 %all-gather.2.cloned.1.call-done = bf16[1536,4096]{1,0:T(8,128)(2,1)} async-done(((bf16[1536,512]{1,0:T(8,128)(2,1)}), bf16[1536,4096]{1,0:T(8,128)(2,1)}) %all-gather.2.cloned.1.call-update) | async-done | bytes 12582928 | tf_op jit(solution)/shard_map/all_gather | solution.py:19
  172.9 0.0 copy-done
  172.9 12.0 %convolution_bitcast_fusion = f32[4096,512]{0,1:T(8,128)} fusion(bf16[1536,4096]{1,0:T(8,128)(2,1)} %all-gather.2.cloned.1.call-done, bf16[1536,512]{1,0:T(8,128)(2,1)S(1)} %copy-done, f32[1536]{0:T(1024)S(1)} %multiply_divide_fusion), kind=kOutput, calls=%fused_computation | convolution fusion | flops 6444810240 | bytes 22550528 | tf_op jit(solution)/shard_map/dot_general | solution.py:21
  184.9 0.0 reduce-scatter.2.cloned.1.call-update
  184.9 98.2 %reduce-scatter.2.cloned.1.call-done = f32[256,512]{0,1:T(8,128)} async-done(((f32[4096,512]{0,1:T(8,128)}), f32[256,512]{0,1:T(8,128)}) %reduce-scatter.2.cloned.1.call-update) | async-done | bytes 524304 | tf_op jit(solution)/shard_map/reduce_scatter | solution.py:20
  (1 shorter events, 0.0 us)
Async XLA Ops:
  6.5 166.4 %copy-start = (bf16[1536,512]{1,0:T(8,128)(2,1)S(1)}, bf16[1536,512]{1,0:T(8,128)(2,1)}, u32[]{:S(2)}) copy-start(bf16[1536,512]{1,0:T(8,128)(2,1)} %param.5) | copy-start | bytes 4718596
  6.5 0.8 copy-start.3
  6.5 2.0 copy-start.2
  6.5 2.0 copy-start.1
  6.5 166.4 %all-gather.2.cloned.1.call-start = ((), (), s32[]{:S(2)}) async-start(), calls=%async_computation.1 | async-start | bytes 14155776 | tf_op jit(solution)/shard_map/all_gather | solution.py:19
  7.3 275.9 %reduce-scatter.2.cloned.1.call-start = ((), (), s32[]{:S(2)}) async-start(), calls=%async_computation.2 | async-start | bytes 8912896 | tf_op jit(solution)/shard_map/reduce_scatter | solution.py:20
Sparse Core Ops, SparseCore 0:
  9.5 163.3 all-gather.1
  185.1 98.0 reduce-scatter.1
where the time goes:
time: 290 us
  waiting for transfers between devices  263 us (91%)
  between operations  13.4 us (5%)
  matrix products  12 us (4%)
    all_gather x1, waiting for transfers between devices, per_device(): gathered = lax.all_gather(densities, 'ga', axis=1, tiled=True)  164 us
    reduce_scatter x1, waiting for transfers between devices, per_device(): lax.psum_scatter(lax.dot_general(gathered, scaled, (((0,), (0,)), ((), ()...  98.2 us
    dot_general x1, matrix products, per_device(): lax.dot_general(gathered, scaled, (((0,), (0,)), ((), ())), preferred_ele...  12 us
  transfers between devices with their start and end apart: 2, of which 2 were waited for; matrix products, arithmetic and copies ran while one was open for 1% of the time, Pallas kernels for 0%

commit v1 on v0

--- a/solution.py
+++ b/solution.py
@@ -16,7 +16,9 @@
     gap = lookup(val_band, val_energy) - lookup(cond_band, cond_energy)
     weight = 4.0 / (gap * math.sqrt(pairs_total))
     scaled = (weight[:, None] * densities.astype(jnp.float32)).astype(jnp.bfloat16)
-    gathered = lax.all_gather(densities, "ga", axis=1, tiled=True)
+    gathered = jnp.concatenate(
+        lax.all_to_all(jnp.stack([densities] * lax.axis_size("ga")), "ga", 0, 0), axis=1
+    )
     owned = lax.psum_scatter(
         lax.dot_general(
             gathered, scaled, (((0,), (0,)), ((), ())), preferred_element_type=jnp.float32

time: 290 us -> 328 us (1.13)
  waiting for transfers between devices: 263 us -> 286 us
  starting transfers between devices: 0.07 us -> 7.68 us
  local copies, waits for them, and re-layouts: 0.01 us -> 7.27 us
    all_gather x1 -> x0, waiting for transfers between devices: 164 us -> none  [per_device(): gathered = lax.all_gather(densities, 'ga', axis=1, tiled=True)]
    all_to_all x0 -> x1, waiting for transfers between devices: none -> 140 us  [per_device(): lax.all_to_all(jnp.stack([densities] * lax.axis_size('ga')), 'ga', 0, 0)]
    reduce_scatter x1, waiting for transfers between devices: 98.2 us -> 146 us  [per_device(): lax.psum_scatter(lax.dot_general(gathered, scaled, (((0,), (0,)), ((), ()...]
    all_to_all x0 -> x1, starting transfers between devices: none -> 7.65 us  [per_device(): lax.all_to_all(jnp.stack([densities] * lax.axis_size('ga')), 'ga', 0, 0)]
    another operation x0 -> x1, local copies, waits for them, and re-layouts: none -> 5.54 us  [per_device(): jnp.stack([densities] * lax.axis_size('ga'))]
  transfers between devices with their start and end apart: 2 -> 2, of which waited for: 2 -> 2; matrix products, arithmetic and copies ran while one was open for 1% -> 0% of each run, Pallas kernels for 0% -> 0%
where the time goes in v1:
time: 328 us
  waiting for transfers between devices  286 us (87%)
  between operations  13.5 us (4%)
  matrix products  12.3 us (4%)
  starting transfers between devices  7.68 us (2%)
  local copies, waits for them, and re-layouts  7.27 us (2%)
    reduce_scatter x1, waiting for transfers between devices, per_device(): lax.psum_scatter(lax.dot_general(gathered, scaled, (((0,), (0,)), ((), ()...  146 us
    all_to_all x1, waiting for transfers between devices, per_device(): lax.all_to_all(jnp.stack([densities] * lax.axis_size('ga')), 'ga', 0, 0)  140 us
    dot_general x1, matrix products, per_device(): lax.dot_general(gathered, scaled, (((0,), (0,)), ((), ())), preferred_ele...  12.3 us
    all_to_all x1, starting transfers between devices, per_device(): lax.all_to_all(jnp.stack([densities] * lax.axis_size('ga')), 'ga', 0, 0)  7.65 us
  transfers between devices with their start and end apart: 2, of which 2 were waited for; matrix products, arithmetic and copies ran while one was open for 0% of the time, Pallas kernels for 0%

profile of v1, /device:TPU:5, one launch (start us, length us, event | category | flops | bytes accessed | tf_op | source)
XLA Modules:
  0.0 327.6 jit_solution(101814148786205377)
XLA Ops:
  6.5 1.7 copy.7
  8.3 5.5 %stack.2 = bf16[8,1536,512]{1,2,0:T(8,128)(2,1)} broadcast(bf16[1536,512]{0,1:T(8,128)(2,1)S(1)} %copy.7), dimensions={1,2} | broadcast | bytes 14155776 | tf_op jit(solution)/shard_map/stack | solution.py:20
  13.8 0.0 copy-start.1
  13.8 0.0 copy-start.4
  13.8 0.0 copy-start.2
  13.8 0.0 copy-start.3
  13.8 0.0 copy-start
  13.8 7.6 %all-to-all-start = ((bf16[8,1536,512]{1,2,0:T(8,128)(2,1)}), bf16[8,1536,512]{1,2,0:T(8,128)(2,1)}, u32[]{:S(2)}, u32[]{:S(2)}) async-start(bf16[8,1536,512]{1,2,0:T(8,128)(2,1)} %stack.2), calls=%async_computation | async-start | bytes 25165824 | tf_op jit(solution)/shard_map/all_to_all | solution.py:20
  21.5 0.0 reduce-scatter.2.cloned.1.call-start
  21.5 0.0 copy-done.1
  21.5 0.0 copy-done.4
  21.5 0.5 select_reduce_fusion.1
  22.0 0.0 copy-done.2
  22.0 0.0 copy-done.3
  22.0 0.5 select_reduce_fusion
  22.6 140.0 %all-to-all-done = bf16[8,1536,512]{1,2,0:T(8,128)(2,1)} async-done(((bf16[8,1536,512]{1,2,0:T(8,128)(2,1)}), bf16[8,1536,512]{1,2,0:T(8,128)(2,1)}, u32[]{:S(2)}, u32[]{:S(2)}) %all-to-all-start) | async-done | bytes 12582944 | tf_op jit(solution)/shard_map/all_to_all | solution.py:20
  162.5 0.0 copy-done
  162.5 12.3 %convolution_bitcast_fusion = f32[4096,512]{0,1:T(8,128)} fusion(bf16[1536,4096]{0,1:T(8,128)(2,1)} %bitcast.1, bf16[1536,512]{1,0:T(8,128)(2,1)S(1)} %copy-done, f32[1536]{0:T(1024)S(1)} %multiply_divide_fusion), kind=kOutput, calls=%fused_computation | convolution fusion | flops 6444810240 | bytes 22550528 | tf_op jit(solution)/shard_map/dot_general | solution.py:23
  174.8 0.0 reduce-scatter.2.cloned.1.call-update
  174.9 145.9 %reduce-scatter.2.cloned.1.call-done = f32[256,512]{0,1:T(8,128)} async-done(((f32[4096,512]{0,1:T(8,128)}), f32[256,512]{0,1:T(8,128)}) %reduce-scatter.2.cloned.1.call-update) | async-done | bytes 524304 | tf_op jit(solution)/shard_map/reduce_scatter | solution.py:22
  (1 shorter events, 0.0 us)
Async XLA Ops:
  13.8 7.7 %copy-start.1 = (s32[1536]{0:T(1024)S(1)}, s32[1536]{0:T(1024)}, u32[]{:S(2)}) copy-start(s32[1536]{0:T(1024)} %param.6) | copy-start | bytes 18436
  13.8 7.7 %copy-start.4 = (f32[128]{0:T(128)S(1)}, f32[128]{0:T(128)}, u32[]{:S(2)}) copy-start(f32[128]{0:T(128)} %param.8) | copy-start | bytes 1540
  13.8 8.2 %copy-start.2 = (s32[1536]{0:T(1024)S(1)}, s32[1536]{0:T(1024)}, u32[]{:S(2)}) copy-start(s32[1536]{0:T(1024)} %param.7) | copy-start | bytes 18436
  13.8 8.2 %copy-start.3 = (f32[256]{0:T(256)S(1)}, f32[256]{0:T(256)}, u32[]{:S(2)}) copy-start(f32[256]{0:T(256)} %param.9) | copy-start | bytes 3076
  13.8 148.7 %copy-start = (bf16[1536,512]{1,0:T(8,128)(2,1)S(1)}, bf16[1536,512]{1,0:T(8,128)(2,1)}, u32[]{:S(2)}) copy-start(bf16[1536,512]{1,0:T(8,128)(2,1)} %param.5) | copy-start | bytes 4718596
  13.8 148.7 %all-to-all-start = ((bf16[8,1536,512]{1,2,0:T(8,128)(2,1)}), bf16[8,1536,512]{1,2,0:T(8,128)(2,1)}, u32[]{:S(2)}, u32[]{:S(2)}) async-start(bf16[8,1536,512]{1,2,0:T(8,128)(2,1)} %stack.2), calls=%async_computation | async-start | bytes 25165824 | tf_op jit(solution)/shard_map/all_to_all | solution.py:20
  21.5 299.3 %reduce-scatter.2.cloned.1.call-start = ((), (), s32[]{:S(2)}) async-start(), calls=%async_computation.2 | async-start | bytes 8912896 | tf_op jit(solution)/shard_map/reduce_scatter | solution.py:22
Sparse Core Ops, SparseCore 0:
  175.0 145.7 reduce-scatter.1
